TPU v7x, 32 devices: a whole 2x2x4 slice. The times are simulated.
32 devices in a mesh: task: 4 (over y, core), param: 8 (over z, x).
Axes of the slice: x: 2, y: 2, z: 4, core: 2. Of those that a mesh axis runs over, the one named last changes fastest.
Arguments:
- params: bfloat16 [16, 512, 4096], P('task', 'param'), may hold values from -6 to 6
- fisher: float32 [16, 512, 4096], P('task', 'param'), may hold values from 3e-06 to 1, as said below
Outputs:
- merged: bfloat16 [512, 4096], P('param')
Inputs may be any that keep to these rules, and one draw needn't show every extreme that they name: `fisher`: every entry is positive; scales differ strongly between tasks and between regions of rows.
All inputs are finite; a program needn't handle non-finite values.
Results may differ from a plain program's by a relative error of at most 0.00045.
Values may be sent and summed in bfloat16 or wider, within the bound.
A program may use at most 64 MiB of HBM per device.

v0:
```python
import functools

import jax
import jax.numpy as jnp
from jax import lax
from jax.experimental import pallas as pl
from jax.experimental.pallas import tpu as pltpu
from jax.sharding import PartitionSpec as P

MESH = pl.DeviceIdType.MESH
LANES = 128
PIECES = 8


def kernel(tasks, groups, params_hbm, fisher_hbm, out, fisher, params, stats, give, take, bound, kept, landed,
           load_f, load_p, stat_send, stat_recv, give_send, give_recv, y_send, y_recv, res_send, res_recv,
           near_send, near_recv):
    count, rows, width = fisher.shape
    chips = tasks // 2
    chunks, chunk = give.shape[2], give.shape[5]
    half, piece = width // 2, width // tasks
    task, param = lax.axis_index("task"), lax.axis_index("param")
    chip, core = task // 2, task % 2
    partner = {"task": chip * 2 + 1 - core, "param": param}

    def chip_at(shift):
        return lax.rem(chip + shift, chips)

    def same_core(shift):
        return {"task": chip_at(shift) * 2 + core, "param": param}

    def member(shift):
        return {"task": task, "param": lax.rem(param + shift, groups)}

    loads_f = [pltpu.make_async_copy(fisher_hbm.at[t], fisher.at[t], load_f.at[t]) for t in range(count)]
    loads_p = [pltpu.make_async_copy(params_hbm.at[t], params.at[t], load_p.at[t]) for t in range(count)]
    for copy in loads_f + loads_p:
        copy.start()

    barrier = pltpu.get_barrier_semaphore()
    greeted = [member(s) for s in range(1, groups)] + [partner] + [same_core(s) for s in range(1, chips)]
    for device in greeted:
        pl.semaphore_signal(barrier, inc=1, device_id=device, device_id_type=MESH)

    tops, sums = [], []
    for t in range(count):
        loads_f[t].wait()

        def over(step, carry, t=t):
            block = fisher[t, :, pl.ds(pl.multiple_of(step * LANES, LANES), LANES)]
            return jnp.maximum(carry[0], block), carry[1] + block

        first = fisher[t, :, 0:LANES]
        top, total = lax.fori_loop(1, width // LANES, over, (first, first), unroll=8)
        tops.append(jnp.max(top, axis=0, keepdims=True))
        sums.append(jnp.sum(total, axis=0, keepdims=True))
    top = jnp.max(jnp.concatenate(tops, axis=0), axis=1, keepdims=True)
    total = jnp.sum(jnp.concatenate(sums, axis=0), axis=1, keepdims=True)
    stats[0, 0:count, :] = jnp.broadcast_to(top, (count, LANES))
    stats[0, count:2 * count, :] = jnp.broadcast_to(total, (count, LANES))

    pl.semaphore_wait(barrier, len(greeted))

    stat_copies = [
        pltpu.make_async_remote_copy(
            src_ref=stats.at[0], dst_ref=stats.at[s], send_sem=stat_send.at[s], recv_sem=stat_recv.at[s],
            device_id=member(s), device_id_type=MESH)
        for s in range(1, groups)
    ]
    for copy in stat_copies:
        copy.start()
    for copy in loads_p:
        copy.wait()
    for copy in stat_copies:
        copy.wait_recv()
    peak, total = stats[0, 0:count, :], stats[0, count:2 * count, :]
    for s in range(1, groups):
        peak = jnp.maximum(peak, stats[s, 0:count, :])
        total = total + stats[s, count:2 * count, :]
    size = float(rows * groups * width)
    gain = size / total
    factor = peak * gain
    low, high = 0.002 * factor, 0.25 * factor
    spread = [
        tuple(jnp.broadcast_to(a[t:t + 1, :], (rows, LANES)) for a in (gain, low, high)) for t in range(count)
    ]

    def partial(side, target, k):
        numers, denoms = [], []
        for part in range(chunk // LANES):
            start = pl.multiple_of(side * half + target * piece + k * chunk + part * LANES, LANES)
            numer = denom = None
            for t in range(count):
                gain_t, low_t, high_t = spread[t]
                info = fisher[t, :, pl.ds(start, LANES)]
                theta = params[t, :, pl.ds(start, LANES)].astype(jnp.float32)
                weight = jnp.minimum(jnp.maximum(info * gain_t, low_t), high_t)
                numer = weight * theta if t == 0 else numer + weight * theta
                denom = weight if t == 0 else denom + weight
            numers.append(numer)
            denoms.append(denom)
        if len(numers) == 1:
            return numers[0], denoms[0]
        return jnp.concatenate(numers, axis=1), jnp.concatenate(denoms, axis=1)

    def put(ref, pair):
        ref[0], ref[1] = pair

    def added(one, two):
        return one[0] + two[0], one[1] + two[1]

    def give_copy(shift, k):
        return pltpu.make_async_remote_copy(
            src_ref=give.at[shift, 0, k], dst_ref=take.at[shift, 0, k], send_sem=give_send.at[shift, k],
            recv_sem=give_recv.at[shift, k], device_id=partner, device_id_type=MESH)

    def y_copy(shift, k):
        return pltpu.make_async_remote_copy(
            src_ref=bound.at[shift - 1, k], dst_ref=landed.at[shift - 1, k], send_sem=y_send.at[shift - 1, k],
            recv_sem=y_recv.at[shift - 1, k], device_id=same_core(shift), device_id_type=MESH)

    def columns(side, target, k):
        return pl.ds(pl.multiple_of(side * half + target * piece + k * chunk, LANES), chunk)

    def res_copy(shift, k):
        where = out.at[:, columns(core, chip, k)]
        return pltpu.make_async_remote_copy(
            src_ref=where, dst_ref=where, send_sem=res_send.at[shift - 1, k], recv_sem=res_recv.at[shift - 1, k],
            device_id=same_core(shift), device_id_type=MESH)

    def near_copy(shift, k):
        where = out.at[:, columns(core, chip_at(chips - shift), k)]
        return pltpu.make_async_remote_copy(
            src_ref=where, dst_ref=where, send_sem=near_send.at[shift, k], recv_sem=near_recv.at[shift, k],
            device_id=partner, device_id_type=MESH)

    away = [(shift, k) for k in range(chunks) for shift in range(1, chips)]
    gives = {}

    def hand_over(shift, k):
        put(give.at[shift, 0, k], partial(1 - core, chip_at(shift), k))
        gives[shift, k] = give_copy(shift, k)
        gives[shift, k].start()

    for shift, k in away:
        hand_over(shift, k)
    for shift, k in away:
        put(bound.at[shift - 1, k], partial(core, chip_at(shift), k))
    y_copies = {}
    for shift, k in away:
        gives[shift, k].wait_recv()
        put(bound.at[shift - 1, k], added(bound.at[shift - 1, k], take.at[shift, 0, k]))
        y_copies[shift, k] = y_copy(shift, k)
        y_copies[shift, k].start()
    for k in range(chunks):
        hand_over(0, k)
    for k in range(chunks):
        put(kept.at[k], partial(core, chip, k))
    for k in range(chunks):
        gives[0, k].wait_recv()
        put(kept.at[k], added(kept.at[k], take.at[0, 0, k]))

    res_copies, near_copies = {}, {}
    for k in range(chunks):
        total = kept[k, 0], kept[k, 1]
        for shift in range(1, chips):
            y_copies[shift, k].wait_recv()
            total = added(total, landed.at[shift - 1, k])
        out[:, columns(core, chip, k)] = (total[0] / total[1]).astype(out.dtype)
        for shift in range(1, chips):
            res_copies[shift, k] = res_copy(shift, k)
            res_copies[shift, k].start()
        near_copies[0, k] = near_copy(0, k)
        near_copies[0, k].start()
    for shift, k in away:
        res_copies[shift, k].wait_recv()
        near_copies[shift, k] = near_copy(shift, k)
        near_copies[shift, k].start()
    for copies in (gives, y_copies, res_copies):
        for copy in copies.values():
            copy.wait_send()
    for copy in stat_copies:
        copy.wait_send()
    for copy in near_copies.values():
        copy.wait()


def local(mesh, params, fisher):
    count, rows, width = fisher.shape
    tasks, groups = mesh.shape["task"], mesh.shape["param"]
    chips, piece = tasks // 2, width // tasks
    chunks = max(1, min(PIECES, piece // LANES))
    chunk = piece // chunks
    far = max(1, chips - 1)
    f32, dma = jnp.float32, pltpu.SemaphoreType.DMA
    return pl.pallas_call(
        functools.partial(kernel, tasks, groups),
        out_shape=pltpu.VMEM((rows, width), jnp.bfloat16),
        in_specs=[pl.BlockSpec(memory_space=pltpu.HBM)] * 2,
        out_specs=pl.BlockSpec(memory_space=pltpu.VMEM),
        scratch_shapes=[
            pltpu.VMEM((count, rows, width), f32),
            pltpu.VMEM((count, rows, width), jnp.bfloat16),
            pltpu.VMEM((groups, 2 * count, LANES), f32),
            pltpu.VMEM((chips, 1, chunks, 2, rows, chunk), f32),
            pltpu.VMEM((chips, 1, chunks, 2, rows, chunk), f32),
            pltpu.VMEM((far, chunks, 2, rows, chunk), f32),
            pltpu.VMEM((chunks, 2, rows, chunk), f32),
            pltpu.VMEM((far, chunks, 2, rows, chunk), f32),
            dma((count,)),
            dma((count,)),
            dma((groups,)),
            dma((groups,)),
            dma((chips, chunks)),
            dma((chips, chunks)),
            dma((far, chunks)),
            dma((far, chunks)),
            dma((far, chunks)),
            dma((far, chunks)),
            dma((chips, chunks)),
            dma((chips, chunks)),
        ],
        compiler_params=pltpu.CompilerParams(collective_id=0, has_side_effects=True),
        name="merge",
    )(params, fisher)


def solution(mesh):
    in_specs = (P("task", "param", None), P("task", "param", None))
    out_specs = P("param", None)
    return jax.shard_map(
        functools.partial(local, mesh), mesh=mesh, in_specs=in_specs, out_specs=out_specs, check_vma=False)
```

profile of v0, /device:TPU:0, one launch (start us, length us, event | category | flops | bytes accessed | tf_op | source)
XLA Modules:
  0.0 30.9 jit_solution(12708952533346922127)
XLA Ops:
  0.0 30.1 %merge.1 = bf16[64,4096]{1,0:T(8,128)(2,1)S(1)} custom-call(bf16[4,64,4096]{2,1,0:T(8,128)(2,1)} %params_hbm.1, f32[4,64,4096]{2,1,0:T(8,128)} %fisher_hbm.1), custom_call_target="tpu_custom_call" | custom-call | tf_op jit(solution)/shard_map/merge/pallas_call | solution.py:196
  30.1 0.8 %copy.4 = bf16[64,4096]{1,0:T(8,128)(2,1)} copy(bf16[64,4096]{1,0:T(8,128)(2,1)S(1)} %merge.1) | data formatting | bytes 1048576
where the time goes:
time: 31.1 us; the launch traced here: 30.9 us
  Pallas kernels  30.1 us (97%)
  local copies, waits for them, and re-layouts  0.8 us (3%)
    pallas_call x1, Pallas kernels, local(): pl.pallas_call(functools.partial(kernel, tasks, groups), out_shape=pltpu....  30.1 us
    unnamed x1, local copies, waits for them, and re-layouts  0.8 us

commit v1 on v0

v1 whole, which is shorter than its diff:
```python
import functools

import jax
import jax.numpy as jnp
from jax import lax
from jax.experimental import pallas as pl
from jax.experimental.pallas import tpu as pltpu
from jax.sharding import PartitionSpec as P

MESH = pl.DeviceIdType.MESH
LANES = 128
SPAN = 126.0
HEAD = 8


def encode(value):
    size = jnp.exp2(jnp.abs(value) * (2.0 * SPAN) - SPAN)
    return jnp.where(value < 0, -size, size).astype(jnp.bfloat16)


def decode(code):
    code = code.astype(jnp.float32)
    size = (jnp.log2(jnp.abs(code)) + SPAN) * (0.5 / SPAN)
    return jnp.where(code < 0, -size, size)


def kernel(tasks, groups, params_hbm, fisher_hbm, out, fisher, params, fisher_in, params_in, mine, stats, sent, landed,
           kept, load_f, load_p, push_f, push_p, in_f, in_p, stat_send, stat_recv, y_send, y_recv, res_send, res_recv,
           near_send, near_recv):
    count, rows, width = fisher.shape
    chips = tasks // 2
    half, piece = width // 2, width // tasks
    chunks = piece // LANES
    task, param = lax.axis_index("task"), lax.axis_index("param")
    chip, core = task // 2, task % 2
    f32 = jnp.float32

    def device(shift, other_core, member):
        to = lax.rem(chip + shift, chips) * 2 + (1 - core if other_core else core)
        return {"task": to, "param": lax.rem(param + member, groups)}

    partner = device(0, True, 0)

    loads_f = [
        [pltpu.make_async_copy(fisher_hbm.at[t, :, pl.ds(h * half, half)], fisher.at[t, :, pl.ds(h * half, half)],
                               load_f.at[t, h]) for h in range(2)] for t in range(count)]
    own = pl.ds(pl.multiple_of(core * half, LANES), half)
    load_params = pltpu.make_async_copy(params_hbm.at[:, :, own], params, load_p)
    for pair in loads_f:
        for copy in pair:
            copy.start()
    load_params.start()

    barrier = pltpu.get_barrier_semaphore()
    greeted = [device(0, other, s) for s in range(groups) for other in (False, True) if other or s]
    greeted += [device(s, False, 0) for s in range(1, chips)]
    for who in greeted:
        pl.semaphore_signal(barrier, inc=1, device_id=who, device_id_type=MESH)

    tops, sums = [], []
    for t in range(count):
        top = total = None
        for h in range(2):
            loads_f[t][h].wait()

            def over(step, carry, t=t, h=h):
                block = fisher[t, :, pl.ds(pl.multiple_of(h * half + step * LANES, LANES), LANES)]
                return jnp.maximum(carry[0], block), carry[1] + block

            if h == 0:
                first = fisher[t, :, 0:LANES]
                top, total = lax.fori_loop(1, half // LANES, over, (first, first), unroll=5)
            else:
                top, total = lax.fori_loop(0, half // LANES, over, (top, total), unroll=4)
        tops.append(jnp.max(top, axis=0, keepdims=True))
        sums.append(jnp.sum(total, axis=0, keepdims=True))
    top = jnp.max(jnp.concatenate(tops, axis=0), axis=1, keepdims=True)
    total = jnp.sum(jnp.concatenate(sums, axis=0), axis=1, keepdims=True)
    column = jnp.broadcast_to(jnp.concatenate([top, total], axis=0), (2 * count, LANES))
    lane = lax.broadcasted_iota(jnp.int32, (2 * count, LANES), 1)
    row = lax.broadcasted_iota(jnp.int32, (2 * count, LANES), 0)
    packed = jnp.sum(jnp.where(lane == row, column, 0.0), axis=0, keepdims=True)
    mine[...] = jnp.broadcast_to(packed, mine.shape)

    pl.semaphore_wait(barrier, len(greeted))

    stat_copies = []
    for s in range(groups - 1, -1, -1):
        for other in (0, 1):
            if not s and not other:
                continue
            stat_copies.append(pltpu.make_async_remote_copy(
                src_ref=mine.at[pl.ds(0, 1)], dst_ref=stats.at[other, pl.ds(s, 1)], send_sem=stat_send.at[other, s],
                recv_sem=stat_recv.at[other, s], device_id=device(0, bool(other), s), device_id_type=MESH))
    for copy in stat_copies:
        copy.start()
    stats[0, 0:1, :] = packed

    def place(shift, k):
        return pl.multiple_of(lax.rem(chip + shift, chips) * piece + k * LANES, LANES)

    order = [(shift, k) for shift in range(1, chips) for k in range(chunks)] + [(0, k) for k in range(chunks)]

    def push_copies(shift, k):
        there = pl.ds(pl.multiple_of((1 - core) * half + place(shift, k), LANES), LANES)
        here = pl.ds(place(shift, k), LANES)
        return [
            pltpu.make_async_remote_copy(
                src_ref=fisher_hbm.at[:, :, there], dst_ref=fisher_in.at[:, :, here], send_sem=push_f.at[shift, k],
                recv_sem=in_f.at[shift, k], device_id=partner, device_id_type=MESH),
            pltpu.make_async_remote_copy(
                src_ref=params_hbm.at[:, :, there], dst_ref=params_in.at[:, :, here], send_sem=push_p.at[shift, k],
                recv_sem=in_p.at[shift, k], device_id=partner, device_id_type=MESH)]

    for shift, k in order:
        for copy in push_copies(shift, k):
            copy.start()

    load_params.wait()
    for copy in stat_copies:
        copy.wait_recv()

    size = float(rows * groups * width)
    spread = []
    for other in (0, 1):
        peaks = jnp.max(stats[other], axis=0, keepdims=True)
        totals = jnp.sum(stats[other], axis=0, keepdims=True)
        for t in range(count):
            peak = jnp.broadcast_to(peaks[:, t:t + 1], (8, LANES))
            gain = size / jnp.broadcast_to(totals[:, count + t:count + t + 1], (8, LANES))
            factor = peak * gain
            spread.append((gain, 0.002 * factor, 0.25 * factor))

    def tall(a):
        return jnp.concatenate([a] * (rows // 8), axis=0)

    def partial(shift, k):
        at = place(shift, k)
        here = pl.ds(at, LANES)
        full = pl.ds(pl.multiple_of(core * half + at, LANES), LANES)
        for copy in push_copies(shift, k):
            copy.wait_recv()
        numer = denom = None
        for other in (0, 1):
            for t in range(count):
                gain, low, high = (tall(a) for a in spread[other * count + t])
                info = fisher_in[t, :, here] if other else fisher[t, :, full]
                theta = (params_in if other else params)[t, :, here].astype(f32)
                weight = jnp.minimum(jnp.maximum(info * gain, low), high)
                numer = weight * theta if numer is None else numer + weight * theta
                denom = weight if denom is None else denom + weight
        return numer, denom

    def y_copy(shift, k):
        return pltpu.make_async_remote_copy(
            src_ref=sent.at[shift - 1, k], dst_ref=landed.at[shift - 1, k], send_sem=y_send.at[shift - 1, k],
            recv_sem=y_recv.at[shift - 1, k], device_id=device(shift, False, 0), device_id_type=MESH)

    def columns(shift, k):
        return pl.ds(pl.multiple_of(core * half + place(shift, k), LANES), LANES)

    def res_copy(shift, k):
        where = out.at[:, columns(0, k)]
        return pltpu.make_async_remote_copy(
            src_ref=where, dst_ref=where, send_sem=res_send.at[shift - 1, k], recv_sem=res_recv.at[shift - 1, k],
            device_id=device(shift, False, 0), device_id_type=MESH)

    def near_copy(shift, k):
        where = out.at[:, columns(chips - shift if shift else 0, k)]
        return pltpu.make_async_remote_copy(
            src_ref=where, dst_ref=where, send_sem=near_send.at[shift, k], recv_sem=near_recv.at[shift, k],
            device_id=partner, device_id_type=MESH)

    head = lax.broadcasted_iota(jnp.int32, (HEAD, LANES), 0)

    for shift in range(1, chips):
        def send(k, carry, shift=shift):
            numer, denom = partial(shift, k)
            mean = numer / denom
            reach = jnp.maximum(jnp.max(jnp.abs(mean), axis=0, keepdims=True) * 1.01, 1e-35)
            reach = reach.astype(jnp.bfloat16).astype(f32)
            most = (jnp.max(denom, axis=0, keepdims=True) * 1.01).astype(jnp.bfloat16).astype(f32)
            box = sent.at[shift - 1, k]
            box[0:rows] = encode(mean * (1.0 / reach))
            box[rows:2 * rows] = encode(2.0 * jnp.sqrt(denom * (1.0 / most)) - 1.0)
            box[2 * rows:2 * rows + HEAD] = jnp.where(head == 0, reach, most).astype(jnp.bfloat16)
            y_copy(shift, k).start()
            return carry

        lax.fori_loop(0, chunks, send, 0)

    def keep(k, carry):
        kept[k, 0], kept[k, 1] = partial(0, k)
        return carry

    lax.fori_loop(0, chunks, keep, 0)

    def finish(k, carry):
        numer, denom = kept[k, 0], kept[k, 1]
        for shift in range(1, chips):
            y_copy(shift, k).wait_recv()
            box = landed.at[shift - 1, k]
            scale = box[2 * rows:2 * rows + HEAD].astype(f32)
            root = decode(box[rows:2 * rows]) * 0.5 + 0.5
            weight = root * root * scale[1:2]
            numer = numer + decode(box[0:rows]) * scale[0:1] * weight
            denom = denom + weight
        out[:, columns(0, k)] = (numer / denom).astype(out.dtype)
        for shift in range(1, chips):
            res_copy(shift, k).start()
        near_copy(0, k).start()
        return carry

    lax.fori_loop(0, chunks, finish, 0)

    for shift in range(1, chips):
        def forward(k, carry, shift=shift):
            res_copy(shift, k).wait_recv()
            near_copy(shift, k).start()
            return carry

        lax.fori_loop(0, chunks, forward, 0)

    for copy in stat_copies:
        copy.wait_send()
    for shift, k in order:
        for copy in push_copies(shift, k):
            copy.wait_send()
        if shift:
            y_copy(shift, k).wait_send()
            res_copy(shift, k).wait_send()
        near_copy(shift, k).wait()


def local(mesh, params, fisher):
    count, rows, width = fisher.shape
    tasks, groups = mesh.shape["task"], mesh.shape["param"]
    chips, piece = tasks // 2, width // tasks
    chunks = piece // LANES
    far = max(1, chips - 1)
    half = width // 2
    f32, bf16, dma = jnp.float32, jnp.bfloat16, pltpu.SemaphoreType.DMA
    return pl.pallas_call(
        functools.partial(kernel, tasks, groups),
        out_shape=pltpu.VMEM((rows, width), bf16),
        in_specs=[pl.BlockSpec(memory_space=pltpu.HBM)] * 2,
        out_specs=pl.BlockSpec(memory_space=pltpu.VMEM),
        scratch_shapes=[
            pltpu.VMEM((count, rows, width), f32),
            pltpu.VMEM((count, rows, half), bf16),
            pltpu.VMEM((count, rows, half), f32),
            pltpu.VMEM((count, rows, half), bf16),
            pltpu.VMEM((8, LANES), f32),
            pltpu.VMEM((2, groups, LANES), f32),
            pltpu.VMEM((far, chunks, 2 * rows + HEAD, LANES), bf16),
            pltpu.VMEM((far, chunks, 2 * rows + HEAD, LANES), bf16),
            pltpu.VMEM((chunks, 2, rows, LANES), f32),
            dma((count, 2)),
            dma(()),
            dma((chips, chunks)),
            dma((chips, chunks)),
            dma((chips, chunks)),
            dma((chips, chunks)),
            dma((2, groups)),
            dma((2, groups)),
            dma((far, chunks)),
            dma((far, chunks)),
            dma((far, chunks)),
            dma((far, chunks)),
            dma((chips, chunks)),
            dma((chips, chunks)),
        ],
        compiler_params=pltpu.CompilerParams(collective_id=0, has_side_effects=True),
        name="merge",
    )(params, fisher)


def solution(mesh):
    in_specs = (P("task", "param", None), P("task", "param", None))
    out_specs = P("param", None)
    return jax.shard_map(
        functools.partial(local, mesh), mesh=mesh, in_specs=in_specs, out_specs=out_specs, check_vma=False)
```

time: 31.1 us -> 24.9 us (0.80)
  Pallas kernels: 30.1 us -> 23.9 us
    pallas_call x1, Pallas kernels: 30.1 us -> 23.9 us  [local(): pl.pallas_call(functools.partial(kernel, tasks, groups), out_shape=pltpu....]
where the time goes in v1:
time: 24.9 us; the launch traced here: 24.7 us
  Pallas kernels  23.9 us (96%)
  local copies, waits for them, and re-layouts  0.8 us (3%)
    pallas_call x1, Pallas kernels, local(): pl.pallas_call(functools.partial(kernel, tasks, groups), out_shape=pltpu....  23.9 us
    unnamed x1, local copies, waits for them, and re-layouts  0.8 us

profile of v1, /device:TPU:0, one launch (start us, length us, event | category | flops | bytes accessed | tf_op | source)
XLA Modules:
  0.0 24.7 jit_solution(343737462525334202)
XLA Ops:
  0.0 23.9 %merge.1 = bf16[64,4096]{1,0:T(8,128)(2,1)S(1)} custom-call(bf16[4,64,4096]{2,1,0:T(8,128)(2,1)} %params_hbm.1, f32[4,64,4096]{2,1,0:T(8,128)} %fisher_hbm.1), custom_call_target="tpu_custom_call" | custom-call | tf_op jit(solution)/shard_map/merge/pallas_call | solution.py:243
  23.9 0.8 %copy.4 = bf16[64,4096]{1,0:T(8,128)(2,1)} copy(bf16[64,4096]{1,0:T(8,128)(2,1)S(1)} %merge.1) | data formatting | bytes 1048576

commit v2 on v1

v2 whole, which is shorter than its diff:
```python
import functools

import jax
import jax.numpy as jnp
from jax import lax
from jax.experimental import pallas as pl
from jax.experimental.pallas import tpu as pltpu
from jax.sharding import PartitionSpec as P

MESH = pl.DeviceIdType.MESH
LANES = 128
SPAN = 126.0
HEAD = 2


def encode(value):
    size = jnp.exp2(jnp.abs(value) * (2.0 * SPAN) - SPAN)
    return jnp.where(value < 0, -size, size).astype(jnp.bfloat16)


def decode(code):
    code = code.astype(jnp.float32)
    size = (jnp.log2(jnp.abs(code)) + SPAN) * (0.5 / SPAN)
    return jnp.where(code < 0, -size, size)


def kernel(tasks, groups, counts, params_hbm, fisher_hbm, out, fisher, params, fisher_in, params_in, mine, stats, sent,
           landed, kept, load_f, load_p, push_f, push_p, in_f, in_p, stat_send, stat_recv, y_send, y_recv, res_send,
           res_recv, near_send, near_recv):
    count, rows, width = fisher.shape
    chips = tasks // 2
    half = width // 2
    starts = (0, counts[0] * chips * LANES)
    task, param = lax.axis_index("task"), lax.axis_index("param")
    chip, core = task // 2, task % 2
    chunks = counts[0] + core * (counts[1] - counts[0])
    f32 = jnp.float32

    def device(shift, other_core, member):
        to = lax.rem(chip + shift, chips) * 2 + (1 - core if other_core else core)
        return {"task": to, "param": lax.rem(param + member, groups)}

    def remote(src, dst, send, recv, who):
        return pltpu.make_async_remote_copy(
            src_ref=src, dst_ref=dst, send_sem=send, recv_sem=recv, device_id=who, device_id_type=MESH)

    def on_each_core(act):
        for c in (0, 1):
            pl.when(core == c)(functools.partial(act, c))

    partner = device(0, True, 0)

    loads_f = [
        [pltpu.make_async_copy(fisher_hbm.at[t, :, pl.ds(h * half, half)], fisher.at[t, :, pl.ds(h * half, half)],
                               load_f.at[t, h]) for h in range(2)] for t in range(count)]
    load_params = pltpu.make_async_copy(params_hbm, params, load_p)
    for pair in loads_f:
        for copy in pair:
            copy.start()

    barrier = pltpu.get_barrier_semaphore()
    greeted = [device(0, other, s) for s in range(groups) for other in (False, True) if other or s]
    greeted += [device(s, False, 0) for s in range(1, chips)]
    for who in greeted:
        pl.semaphore_signal(barrier, inc=1, device_id=who, device_id_type=MESH)

    tops, sums = [], []
    for t in range(count):
        top = total = None
        for h in range(2):
            loads_f[t][h].wait()

            def over(step, carry, t=t, h=h):
                block = fisher[t, :, pl.ds(pl.multiple_of(h * half + step * LANES, LANES), LANES)]
                return jnp.maximum(carry[0], block), carry[1] + block

            if h == 0:
                first = fisher[t, :, 0:LANES]
                top, total = lax.fori_loop(1, half // LANES, over, (first, first), unroll=5)
            else:
                top, total = lax.fori_loop(0, half // LANES, over, (top, total), unroll=4)
        tops.append(jnp.max(top, axis=0, keepdims=True))
        sums.append(jnp.sum(total, axis=0, keepdims=True))
    load_params.start()
    top = jnp.max(jnp.concatenate(tops, axis=0), axis=1, keepdims=True)
    total = jnp.sum(jnp.concatenate(sums, axis=0), axis=1, keepdims=True)
    column = jnp.broadcast_to(jnp.concatenate([top, total], axis=0), (2 * count, LANES))
    lane = lax.broadcasted_iota(jnp.int32, (2 * count, LANES), 1)
    row = lax.broadcasted_iota(jnp.int32, (2 * count, LANES), 0)
    packed = jnp.sum(jnp.where(lane == row, column, 0.0), axis=0, keepdims=True)
    mine[...] = jnp.broadcast_to(packed, mine.shape)

    pl.semaphore_wait(barrier, len(greeted))

    for s in range(groups - 1, -1, -1):
        for other in (0, 1):
            if s or other:
                remote(mine.at[pl.ds(0, 1)], stats.at[pl.ds(other * groups + s, 1)], stat_send, stat_recv,
                       device(0, bool(other), s)).start()
    stats[0:1, :] = packed
    others = stats.at[pl.ds(1, 2 * groups - 1)]
    stat_all = remote(others, others, stat_send, stat_recv, partner)

    def block(c, shift):
        size = counts[c] * LANES
        return pl.multiple_of(lax.rem(chip + shift, chips) * size, LANES), size

    def push_copies(c, shift):
        at, size = block(c, shift)
        there = pl.ds(pl.multiple_of(starts[c] + at, LANES), size)
        here = pl.ds(at, size)
        return [remote(fisher_hbm.at[:, :, there], fisher_in.at[:, :, here], push_f, in_f.at[shift], partner),
                remote(params_hbm.at[:, :, there], params_in.at[:, :, here], push_p, in_p.at[shift], partner)]

    turns = list(range(1, chips)) + [0]

    @on_each_core
    def _(c):
        for shift in turns:
            for copy in push_copies(1 - c, shift):
                copy.start()

    load_params.wait()
    stat_all.wait_recv()

    size = float(rows * groups * width)
    spread = []
    for other in (0, 1):
        told = stats[other * groups:(other + 1) * groups]
        peaks = jnp.max(told, axis=0, keepdims=True)
        totals = jnp.sum(told, axis=0, keepdims=True)
        for t in range(count):
            peak = jnp.broadcast_to(peaks[:, t:t + 1], (8, LANES))
            gain = size / jnp.broadcast_to(totals[:, count + t:count + t + 1], (8, LANES))
            factor = peak * gain
            spread.append((gain, 0.002 * factor, 0.25 * factor))

    def tall(a):
        return jnp.concatenate([a] * (rows // 8), axis=0)

    def place(shift, k):
        return pl.multiple_of((lax.rem(chip + shift, chips) * chunks + k) * LANES, LANES)

    def columns(shift, k):
        return pl.ds(pl.multiple_of(core * starts[1] + place(shift, k), LANES), LANES)

    def pushed(shift):
        @on_each_core
        def _(c):
            for copy in push_copies(c, shift):
                copy.wait_recv()

    def partial(shift, k):
        here, full = pl.ds(place(shift, k), LANES), columns(shift, k)
        numer = denom = None
        for other in (0, 1):
            at = here if other else full
            for t in range(count):
                gain, low, high = (tall(a) for a in spread[other * count + t])
                info = (fisher_in if other else fisher)[t, :, at]
                theta = (params_in if other else params)[t, :, at].astype(f32)
                weight = jnp.minimum(jnp.maximum(info * gain, low), high)
                numer = weight * theta if numer is None else numer + weight * theta
                denom = weight if denom is None else denom + weight
        return numer, denom

    def y_copy(shift, k):
        return remote(sent.at[shift - 1, k], landed.at[shift - 1, k], y_send, y_recv.at[shift - 1, k],
                      device(shift, False, 0))

    def res_copy(shift, k):
        where = out.at[:, columns(0, k)]
        return remote(where, where, res_send, res_recv.at[shift - 1, k], device(shift, False, 0))

    def near_copy(shift, k):
        where = out.at[:, columns(chips - shift if shift else 0, k)]
        return remote(where, where, near_send, near_recv, partner)

    head = lax.broadcasted_iota(jnp.int32, (HEAD, LANES), 0)

    for shift in range(1, chips):
        pushed(shift)

        def send(k, carry, shift=shift):
            numer, denom = partial(shift, k)
            mean = numer / denom
            reach = jnp.maximum(jnp.max(jnp.abs(mean), axis=0, keepdims=True) * 1.01, 1e-35)
            reach = reach.astype(jnp.bfloat16).astype(f32)
            most = (jnp.max(denom, axis=0, keepdims=True) * 1.01).astype(jnp.bfloat16).astype(f32)
            box = sent.at[shift - 1, k]
            box[0:rows] = encode(mean * (1.0 / reach))
            box[rows:2 * rows] = encode(2.0 * jnp.sqrt(denom * (1.0 / most)) - 1.0)
            box[2 * rows:2 * rows + HEAD] = jnp.where(head == 0, reach, most).astype(jnp.bfloat16)
            y_copy(shift, k).start()
            return carry

        lax.fori_loop(0, chunks, send, 0)

    pushed(0)

    def keep(k, carry):
        kept[k, 0], kept[k, 1] = partial(0, k)
        return carry

    lax.fori_loop(0, chunks, keep, 0)

    def finish(k, carry):
        numer, denom = kept[k, 0], kept[k, 1]
        for shift in range(1, chips):
            y_copy(shift, k).wait_recv()
            box = landed.at[shift - 1, k]
            scale = box[2 * rows:2 * rows + HEAD].astype(f32)
            root = decode(box[rows:2 * rows]) * 0.5 + 0.5
            weight = root * root * scale[1:2]
            numer = numer + decode(box[0:rows]) * scale[0:1] * weight
            denom = denom + weight
        out[:, columns(0, k)] = (numer / denom).astype(out.dtype)
        for shift in range(1, chips):
            res_copy(shift, k).start()
        near_copy(0, k).start()
        return carry

    lax.fori_loop(0, chunks, finish, 0)

    for shift in range(1, chips):
        def forward(k, carry, shift=shift):
            res_copy(shift, k).wait_recv()
            near_copy(shift, k).start()
            return carry

        lax.fori_loop(0, chunks, forward, 0)

    stat_all.wait_send()

    @on_each_core
    def _(c):
        def strip(ref, size):
            return ref.at[:, pl.ds(0, size * LANES)]

        def whole(src, send):
            return remote(src, src, send, near_recv, partner)

        given = pl.ds(0, chips * counts[1 - c] * LANES)
        whole(fisher_hbm.at[:, :, given], push_f).wait_send()
        whole(params_hbm.at[:, :, given], push_p).wait_send()
        whole(sent.at[:, pl.ds(0, counts[c])], y_send).wait_send()
        whole(strip(out, (chips - 1) * counts[c]), res_send).wait_send()
        whole(strip(out, chips * counts[c]), near_send).wait_send()
        whole(strip(out, chips * counts[1 - c]), near_send).wait_recv()


def local(mesh, params, fisher):
    count, rows, width = fisher.shape
    tasks, groups = mesh.shape["task"], mesh.shape["param"]
    chips, chunks = tasks // 2, width // tasks // LANES
    counts = (chunks - chunks // 8, chunks + chunks // 8)
    most, far = counts[1], max(1, chips - 1)
    side = most * chips * LANES
    f32, bf16, dma = jnp.float32, jnp.bfloat16, pltpu.SemaphoreType.DMA
    return pl.pallas_call(
        functools.partial(kernel, tasks, groups, counts),
        out_shape=pltpu.VMEM((rows, width), bf16),
        in_specs=[pl.BlockSpec(memory_space=pltpu.HBM)] * 2,
        out_specs=pl.BlockSpec(memory_space=pltpu.VMEM),
        scratch_shapes=[
            pltpu.VMEM((count, rows, width), f32),
            pltpu.VMEM((count, rows, width), bf16),
            pltpu.VMEM((count, rows, side), f32),
            pltpu.VMEM((count, rows, side), bf16),
            pltpu.VMEM((8, LANES), f32),
            pltpu.VMEM((2 * groups, LANES), f32),
            pltpu.VMEM((far, most, 2 * rows + HEAD, LANES), bf16),
            pltpu.VMEM((far, most, 2 * rows + HEAD, LANES), bf16),
            pltpu.VMEM((most, 2, rows, LANES), f32),
            dma((count, 2)),
            dma(()),
            dma(()),
            dma(()),
            dma((chips,)),
            dma((chips,)),
            dma(()),
            dma(()),
            dma(()),
            dma((far, most)),
            dma(()),
            dma((far, most)),
            dma(()),
            dma(()),
        ],
        compiler_params=pltpu.CompilerParams(collective_id=0, has_side_effects=True),
        name="merge",
    )(params, fisher)


def solution(mesh):
    in_specs = (P("task", "param", None), P("task", "param", None))
    out_specs = P("param", None)
    return jax.shard_map(
        functools.partial(local, mesh), mesh=mesh, in_specs=in_specs, out_specs=out_specs, check_vma=False)
```

time: 24.9 us -> 23.1 us (0.928)
  Pallas kernels: 23.9 us -> 22.2 us
    pallas_call x1, Pallas kernels: 23.9 us -> 22.2 us  [local(): pl.pallas_call(functools.partial(kernel, tasks, groups, counts), out_shap...]
where the time goes in v2:
time: 23.1 us; the launch traced here: 23 us
  Pallas kernels  22.2 us (96%)
  local copies, waits for them, and re-layouts  0.8 us (3%)
    pallas_call x1, Pallas kernels, local(): pl.pallas_call(functools.partial(kernel, tasks, groups, counts), out_shap...  22.2 us
    unnamed x1, local copies, waits for them, and re-layouts  0.8 us

profile of v2, /device:TPU:0, one launch (start us, length us, event | category | flops | bytes accessed | tf_op | source)
XLA Modules:
  0.0 23.0 jit_solution(8689713636989160993)
XLA Ops:
  0.0 22.2 %merge.1 = bf16[64,4096]{1,0:T(8,128)(2,1)S(1)} custom-call(bf16[4,64,4096]{2,1,0:T(8,128)(2,1)} %params_hbm.1, f32[4,64,4096]{2,1,0:T(8,128)} %fisher_hbm.1), custom_call_target="tpu_custom_call" | custom-call | tf_op jit(solution)/shard_map/merge/pallas_call | solution.py:260
  22.2 0.8 %copy.4 = bf16[64,4096]{1,0:T(8,128)(2,1)} copy(bf16[64,4096]{1,0:T(8,128)(2,1)S(1)} %merge.1) | data formatting | bytes 1048576
